TPU v7x, 32 devices: a whole 2x2x4 slice. The times are simulated.
32 devices in a mesh: row: 4 (over z), col: 2 (over x), dp: 4 (over y, core).
Axes of the slice: x: 2, y: 2, z: 4, core: 2. Of those that a mesh axis runs over, the one named last changes fastest.
Arguments:
- tokens: bfloat16 [1536, 6144], P('dp', 'row'), parts along dimension 0, may hold values from -120 to 120
- norm_gain: float32 [6144], P('row'), may hold values from 0.25 to 1.75
- qkv_weight: bfloat16 [6144, 3, 3072], P('row', None, 'col'), may hold values from -2.5 to 2.5
- out_weight: bfloat16 [3072, 6144], P('col', 'row'), may hold values from -0.109375 to 0.109375
Outputs:
- projected: bfloat16 [1536, 6144], P('dp', 'row'), parts along dimension 0
There are 4 independent parts, one for each index of `dp`. A program takes and returns all parts, laid end to end along the dimension named above; an argument that names none is the same for every part. Nothing has to cross between parts.
All inputs are finite; a program needn't handle non-finite values.
Results may differ from a plain program's by a relative error of at most 0.025.
Values may be sent and summed in bfloat16 or wider, within the bound.
A program may use at most 64 MiB of HBM per device.

v0:
```python
import math
import jax
import jax.numpy as jnp
from jax import lax
from jax.sharding import PartitionSpec as P

K = 128
EPSILON = 1e-05


def attend(queries, key_rows, value_rows):
    query_total = queries.shape[0]
    head_count = queries.shape[1] // K
    scaling = 1.0 / math.sqrt(K)
    split_keys = key_rows.reshape(key_rows.shape[0], head_count, K)
    split_values = value_rows.reshape(value_rows.shape[0], head_count, K)
    split_queries = queries.reshape(query_total, head_count, K)
    scores = (
        jnp.einsum("qhd,khd->hqk", split_queries, split_keys, preferred_element_type=jnp.float32)
        * scaling
    )
    largest = jnp.max(scores, axis=2, keepdims=True)
    exponent = jnp.exp(scores - largest)
    softmax_weights = (exponent / jnp.sum(exponent, axis=2, keepdims=True)).astype(jnp.bfloat16)
    mixed = jnp.einsum(
        "hqk,khd->qhd", softmax_weights, split_values, preferred_element_type=jnp.float32
    )
    result = mixed.astype(jnp.bfloat16)
    return result.reshape(query_total, head_count * K)


def shards(tokens, norm_gain, qkv_weight, out_weight):
    row_count, block_width = tokens.shape
    full_width = block_width * lax.axis_size("row")
    values = tokens.astype(jnp.float32)
    totals, squares = lax.psum(
        (jnp.sum(values, axis=1, keepdims=True), jnp.sum(values * values, axis=1, keepdims=True)),
        "row",
    )
    average = totals / full_width
    variance = squares / full_width - average * average
    centered = values - average
    normed = (centered * lax.rsqrt(variance + EPSILON) * norm_gain).astype(jnp.bfloat16)
    head_columns = qkv_weight.shape[2]
    partial_value = jnp.dot(
        normed,
        qkv_weight.reshape(block_width, 3 * head_columns),
        preferred_element_type=jnp.float32,
    )
    summed = lax.psum(partial_value.astype(jnp.bfloat16), "row").reshape(row_count, 3, head_columns)
    attended = attend(summed[:, 0], summed[:, 1], summed[:, 2])
    partial_out = jnp.dot(attended, out_weight, preferred_element_type=jnp.float32)
    return lax.psum(partial_out.astype(jnp.bfloat16), "col")


def solution(mesh):
    in_specs = (P("dp", "row"), P("row"), P("row", None, "col"), P("col", "row"))
    out_specs = P("dp", "row")
    return jax.shard_map(shards, mesh=mesh, in_specs=in_specs, out_specs=out_specs, check_vma=False)
```

profile of v0, /device:TPU:0, one launch (start us, length us, event | category | flops | bytes accessed | tf_op | source)
XLA Modules:
  0.0 253.6 jit_solution(16139016888201354875)
XLA Ops:
  6.5 0.0 all-reduce.4.cloned.1.call-start
  6.5 1.7 convert_reduce_fusion
  8.3 0.0 copy-start
  8.3 18.6 %copy.7 = bf16[1536,3,1536]{0,2,1:T(8,128)(2,1)} copy(bf16[1536,3,1536]{2,0,1:T(8,128)(2,1)} %param.6) | data formatting | bytes 28311552 | tf_op args[2]
  26.9 13.5 %all-reduce = (f32[384,1]{0,1:T(1,128)S(1)}, f32[384,1]{0,1:T(1,128)S(1)}) all-reduce(f32[384,1]{0,1:T(1,128)S(1)} %broadcast_in_dim.4, f32[384,1]{0,1:T(1,128)S(1)} %broadcast_in_dim.10), channel_id=1, replica_groups=mesh['row'=4,'col'=2,'dp'=4] {'row'}, use_global_device_ids=true, to_apply=%region_1.0 | all-reduce | flops 768 | bytes 6144 | tf_op jit(solution)/shard_map/psum | solution.py:36
  40.4 0.0 copy-done
  40.4 9.4 %convolution_convert_fusion = bf16[384,4608]{1,0:T(8,128)(2,1)S(1)} fusion(bf16[1536,4608]{0,1:T(8,128)(2,1)} %bitcast.16, bf16[384,1536]{1,0:T(8,128)(2,1)} %param.4, f32[1536]{0:T(1024)S(1)} %copy-done, f32[384]{0:T(512)S(1)} %get-tuple-element.8, f32[384]{0:T(512)S(1)} %get-tuple-element.7), kind=kOutput, calls=%fused_computation.3 | convolution fusion | flops 5440536576 | bytes 18883584 | tf_op jit(solution)/shard_map/dot_general | solution.py:45
  49.9 3.6 %copy.8 = bf16[384,4608]{0,1:T(8,128)(2,1)} copy(bf16[384,4608]{1,0:T(8,128)(2,1)S(1)} %convolution_convert_fusion) | data formatting | bytes 7077888 | tf_op jit(solution)/shard_map/convert_element_type | solution.py:50
  53.5 0.0 all-reduce.4.cloned.1.call-update
  53.5 0.0 all-reduce.6.cloned.1.call-start
  53.6 132.1 %all-reduce.4.cloned.1.call-done = bf16[384,3,1536]{0,2,1:T(8,128)(2,1)} async-done(((bf16[384,3,1536]{0,2,1:T(8,128)(2,1)}), bf16[384,3,1536]{0,2,1:T(8,128)(2,1)}) %all-reduce.4.cloned.1.call-update) | async-done | bytes 3538960 | tf_op jit(solution)/shard_map/psum | solution.py:50
  185.7 2.3 fusion.18
  188.0 4.9 %fusion.19 = (f32[12,384]{1,0:T(8,128)}, f32[12,384,384]{1,2,0:T(8,128)}) fusion(bf16[384,12,128]{0,2,1:T(8,128)(2,1)S(1)} %bitcast.20, bf16[384,12,128]{0,2,1:T(8,128)(2,1)S(1)} %bitcast.19), kind=kOutput, calls=%fused_computation.25 | convolution fusion | flops 458293632 | bytes 9455616 | tf_op jit(solution)/shard_map/sub | solution.py:23
  192.9 4.0 %fusion.10 = bf16[12,128,384]{2,1,0:T(8,128)(2,1)S(1)} fusion(bf16[384,12,128]{0,2,1:T(8,128)(2,1)S(1)} %bitcast.18, f32[12,384,384]{1,2,0:T(8,128)} %get-tuple-element.15, f32[12,384]{1,0:T(8,128)} %get-tuple-element.14), kind=kOutput, calls=%fused_computation.16 | convolution fusion | flops 457113600 | bytes 9455616 | tf_op jit(solution)/shard_map/hqk,khd->qhd/dot_general | solution.py:25
  196.9 5.4 %convolution_convert_fusion.1 = bf16[384,1536]{1,0:T(8,128)(2,1)} fusion(bf16[384,1536]{0,1:T(8,128)(2,1)S(1)} %bitcast.21, bf16[1536,1536]{1,0:T(8,128)(2,1)} %param.7), kind=kOutput, calls=%fused_computation.11 | convolution fusion | flops 1812529152 | bytes 7077888 | tf_op jit(solution)/shard_map/dot_general | solution.py:52
  202.3 0.0 all-reduce.6.cloned.1.call-update
  202.3 42.1 %all-reduce.6.cloned.1.call-done = bf16[384,1536]{1,0:T(8,128)(2,1)} async-done(((bf16[384,1536]{1,0:T(8,128)(2,1)}), bf16[384,1536]{1,0:T(8,128)(2,1)}) %all-reduce.6.cloned.1.call-update) | async-done | bytes 1179664 | tf_op jit(solution)/shard_map/psum | solution.py:53
  244.4 2.4 copy.17
  (3 shorter events, 0.0 us)
Async XLA Ops:
  6.5 179.1 %all-reduce.4.cloned.1.call-start = ((), (), s32[]{:S(2)}) async-start(), calls=%async_computation | async-start | bytes 7077888 | tf_op jit(solution)/shard_map/psum | solution.py:50
  8.3 32.1 %copy-start = (f32[1536]{0:T(1024)S(1)}, f32[1536]{0:T(1024)}, u32[]{:S(2)}) copy-start(f32[1536]{0:T(1024)} %param.5) | copy-start | bytes 18436
  53.5 190.9 %all-reduce.6.cloned.1.call-start = ((), (), s32[]{:S(2)}) async-start(), calls=%async_computation.1 | async-start | bytes 2359296 | tf_op jit(solution)/shard_map/psum | solution.py:53
Sparse Core Ops, SparseCore 0:
  53.6 131.9 all-reduce.3
  202.4 41.9 all-reduce.5
where the time goes:
time: 254 us
  waiting for transfers between devices  174 us (69%)
  local copies, waits for them, and re-layouts  27 us (11%)
  matrix products  23.7 us (9%)
  blocking collectives  13.5 us (5%)
  between operations  13.4 us (5%)
    psum x1, waiting for transfers between devices, shards(): lax.psum(partial_value.astype(jnp.bfloat16), 'row')  132 us
    psum x1, waiting for transfers between devices, shards(): return lax.psum(partial_out.astype(jnp.bfloat16), 'col')  42.1 us
    unnamed x4, local copies, waits for them, and re-layouts  21 us
    psum x1, blocking collectives, shards(): lax.psum((jnp.sum(values, axis=1, keepdims=True), jnp.sum(values * values...  13.5 us
    dot_general x1, matrix products, shards(): jnp.dot(normed, qkv_weight.reshape(block_width, 3 * head_columns), prefer...  9.45 us
    dot_general x1, matrix products, shards(): jnp.dot(attended, out_weight, preferred_element_type=jnp.float32)  5.37 us
  transfers between devices with their start and end apart: 2, of which 2 were waited for; matrix products, arithmetic and copies ran while one was open for 0% of the time, Pallas kernels for 0%

commit v1 on v0

--- a/solution.py
+++ b/solution.py
@@ -50,7 +50,7 @@
     summed = lax.psum(partial_value.astype(jnp.bfloat16), "row").reshape(row_count, 3, head_columns)
     attended = attend(summed[:, 0], summed[:, 1], summed[:, 2])
     partial_out = jnp.dot(attended, out_weight, preferred_element_type=jnp.float32)
-    return lax.psum(partial_out.astype(jnp.bfloat16), "col")
+    return jnp.sum(lax.all_gather(partial_out.astype(jnp.bfloat16), "col"), 0)
 
 
 def solution(mesh):

time: 254 us -> 248 us (0.976)
  waiting for transfers between devices: 174 us -> 167 us
  other arithmetic: 1.76 us -> 5.19 us
    psum x1 -> x0, waiting for transfers between devices: 42.1 us -> none  [shards(): return lax.psum(partial_out.astype(jnp.bfloat16), 'col')]
    all_gather x0 -> x1, waiting for transfers between devices: none -> 35.2 us  [shards(): return jnp.sum(lax.all_gather(partial_out.astype(jnp.bfloat16), 'col'), 0)]
    reduce_sum x0 -> x1, other arithmetic: none -> 3.43 us  [shards(): return jnp.sum(lax.all_gather(partial_out.astype(jnp.bfloat16), 'col'), 0)]
    unnamed x4 -> x3, local copies, waits for them, and re-layouts: 21 us -> 18.7 us
where the time goes in v1:
time: 248 us
  waiting for transfers between devices  167 us (67%)
  local copies, waits for them, and re-layouts  24.6 us (10%)
  matrix products  23.7 us (10%)
  blocking collectives  13.5 us (5%)
  between operations  13.4 us (5%)
  other arithmetic  5.19 us (2%)
    psum x1, waiting for transfers between devices, shards(): lax.psum(partial_value.astype(jnp.bfloat16), 'row')  132 us
    all_gather x1, waiting for transfers between devices, shards(): return jnp.sum(lax.all_gather(partial_out.astype(jnp.bfloat16), 'col'), 0)  35.2 us
    unnamed x3, local copies, waits for them, and re-layouts  18.7 us
    psum x1, blocking collectives, shards(): lax.psum((jnp.sum(values, axis=1, keepdims=True), jnp.sum(values * values...  13.5 us
    dot_general x1, matrix products, shards(): jnp.dot(normed, qkv_weight.reshape(block_width, 3 * head_columns), prefer...  9.45 us
    dot_general x1, matrix products, shards(): jnp.dot(attended, out_weight, preferred_element_type=jnp.float32)  5.37 us
  transfers between devices with their start and end apart: 2, of which 2 were waited for; matrix products, arithmetic and copies ran while one was open for 0% of the time, Pallas kernels for 0%

profile of v1, /device:TPU:0, one launch (start us, length us, event | category | flops | bytes accessed | tf_op | source)
XLA Modules:
  0.0 247.7 jit_solution(9701323430951590879)
XLA Ops:
  6.5 0.0 all-reduce.3.cloned.1.call-start
  6.5 1.7 convert_reduce_fusion
  8.3 0.0 copy-start
  8.3 18.6 %copy.7 = bf16[1536,3,1536]{0,2,1:T(8,128)(2,1)} copy(bf16[1536,3,1536]{2,0,1:T(8,128)(2,1)} %param.6) | data formatting | bytes 28311552 | tf_op args[2]
  26.9 13.5 %all-reduce = (f32[384,1]{0,1:T(1,128)S(1)}, f32[384,1]{0,1:T(1,128)S(1)}) all-reduce(f32[384,1]{0,1:T(1,128)S(1)} %broadcast_in_dim.4, f32[384,1]{0,1:T(1,128)S(1)} %broadcast_in_dim.10), channel_id=1, replica_groups=mesh['row'=4,'col'=2,'dp'=4] {'row'}, use_global_device_ids=true, to_apply=%region_1.0 | all-reduce | flops 768 | bytes 6144 | tf_op jit(solution)/shard_map/psum | solution.py:36
  40.4 0.0 copy-done
  40.4 9.4 %convolution_convert_fusion = bf16[384,4608]{1,0:T(8,128)(2,1)S(1)} fusion(bf16[1536,4608]{0,1:T(8,128)(2,1)} %bitcast.17, bf16[384,1536]{1,0:T(8,128)(2,1)} %param.4, f32[1536]{0:T(1024)S(1)} %copy-done, f32[384]{0:T(512)S(1)} %get-tuple-element.8, f32[384]{0:T(512)S(1)} %get-tuple-element.7), kind=kOutput, calls=%fused_computation.3 | convolution fusion | flops 5440536576 | bytes 18883584 | tf_op jit(solution)/shard_map/dot_general | solution.py:45
  49.9 3.6 %copy.8 = bf16[384,4608]{0,1:T(8,128)(2,1)} copy(bf16[384,4608]{1,0:T(8,128)(2,1)S(1)} %convolution_convert_fusion) | data formatting | bytes 7077888 | tf_op jit(solution)/shard_map/convert_element_type | solution.py:50
  53.5 0.0 all-reduce.3.cloned.1.call-update
  53.5 0.0 all-gather.3.cloned.1.call-start
  53.6 132.1 %all-reduce.3.cloned.1.call-done = bf16[384,3,1536]{0,2,1:T(8,128)(2,1)} async-done(((bf16[384,3,1536]{0,2,1:T(8,128)(2,1)}), bf16[384,3,1536]{0,2,1:T(8,128)(2,1)}) %all-reduce.3.cloned.1.call-update) | async-done | bytes 3538960 | tf_op jit(solution)/shard_map/psum | solution.py:50
  185.7 2.3 fusion.18
  188.0 4.9 %fusion.19 = (f32[12,384]{1,0:T(8,128)}, f32[12,384,384]{1,2,0:T(8,128)}) fusion(bf16[384,12,128]{0,2,1:T(8,128)(2,1)S(1)} %bitcast.22, bf16[384,12,128]{0,2,1:T(8,128)(2,1)S(1)} %bitcast.21), kind=kOutput, calls=%fused_computation.25 | convolution fusion | flops 458293632 | bytes 9455616 | tf_op jit(solution)/shard_map/sub | solution.py:23
  192.9 4.0 %fusion.10 = bf16[12,128,384]{2,1,0:T(8,128)(2,1)S(1)} fusion(bf16[384,12,128]{0,2,1:T(8,128)(2,1)S(1)} %bitcast.20, f32[12,384,384]{1,2,0:T(8,128)} %get-tuple-element.15, f32[12,384]{1,0:T(8,128)} %get-tuple-element.14), kind=kOutput, calls=%fused_computation.16 | convolution fusion | flops 457113600 | bytes 9455616 | tf_op jit(solution)/shard_map/hqk,khd->qhd/dot_general | solution.py:25
  196.9 5.4 %convolution_convert_fusion.1 = bf16[384,1536]{1,0:T(8,128)(2,1)} fusion(bf16[384,1536]{0,1:T(8,128)(2,1)S(1)} %bitcast.23, bf16[1536,1536]{1,0:T(8,128)(2,1)} %param.7), kind=kOutput, calls=%fused_computation.11 | convolution fusion | flops 1812529152 | bytes 7077888 | tf_op jit(solution)/shard_map/dot_general | solution.py:52
  202.3 0.0 all-gather.3.cloned.1.call-update
  202.3 35.2 %all-gather.3.cloned.1.call-done = bf16[768,1536]{1,0:T(8,128)(2,1)} async-done(((bf16[384,1536]{1,0:T(8,128)(2,1)}), bf16[768,1536]{1,0:T(8,128)(2,1)}) %all-gather.3.cloned.1.call-update) | async-done | bytes 2359312 | tf_op jit(solution)/shard_map/all_gather | solution.py:53
  237.5 3.4 %reduce_sum.42 = bf16[384,1536]{1,0:T(8,128)(2,1)} reduce(bf16[2,384,1536]{2,1,0:T(8,128)(2,1)} %bitcast.19, bf16[]{:T(256)} %constant.13.clone.1), dimensions={0}, to_apply=%region_7.0 | reduce | flops 589824 | bytes 3538946 | tf_op jit(solution)/shard_map/reduce_sum | solution.py:53
  (3 shorter events, 0.0 us)
Async XLA Ops:
  6.5 179.1 %all-reduce.3.cloned.1.call-start = ((), (), s32[]{:S(2)}) async-start(), calls=%async_computation | async-start | bytes 7077888 | tf_op jit(solution)/shard_map/psum | solution.py:50
  8.3 32.1 %copy-start = (f32[1536]{0:T(1024)S(1)}, f32[1536]{0:T(1024)}, u32[]{:S(2)}) copy-start(f32[1536]{0:T(1024)} %param.5) | copy-start | bytes 18436
  53.5 183.9 %all-gather.3.cloned.1.call-start = ((), (), s32[]{:S(2)}) async-start(), calls=%async_computation.1 | async-start | bytes 3538944 | tf_op jit(solution)/shard_map/all_gather | solution.py:53
Sparse Core Ops, SparseCore 0:
  53.6 131.9 all-reduce.2
  202.4 35.0 all-gather.2
